TPU v7x, 32 devices: a 4x4x1 block of a 4x4x8 slice. The times are simulated.
32 devices in a mesh: dp: 1 (over z), pool: 4 (over y), ep: 8 (over x, core).
Axes of the slice: x: 4, y: 4, z: 1, core: 2. Of those that a mesh axis runs over, the one named last changes fastest.
The devices are a block of a 4x4x8 slice.
Arguments:
- hidden: bfloat16 [2048, 1536], P(('dp', 'ep'))
- k_cache: bfloat16 [2, 2048, 128, 2, 128], P(None, ('dp', 'ep'))
- v_cache: bfloat16 [2, 2048, 128, 2, 128], P(None, ('dp', 'ep'))
- lengths: int32 [2048], P(('dp', 'ep'))
- expert_ids: int32 [2, 2048, 4], P(None, ('dp', 'ep'))
- w_query: bfloat16 [2, 1536, 1536], replicated
- w_key: bfloat16 [2, 1536, 256], replicated
- w_value: bfloat16 [2, 1536, 256], replicated
- w_out: bfloat16 [2, 1536, 1536], replicated
- w_router: float32 [2, 1536, 16], replicated
- w_gate: bfloat16 [2, 16, 1536, 2688], P(None, 'ep')
- w_up: bfloat16 [2, 16, 1536, 2688], P(None, 'ep')
- w_down: bfloat16 [2, 16, 2688, 1536], P(None, 'ep')
Outputs:
- output: bfloat16 [2048, 1536], P(('dp', 'ep'))
All inputs are finite; a program needn't handle non-finite values.
Results may differ from a plain program's by a relative error of at most 0.0185129.
Values are sent between devices in bfloat16 or wider.
A program may use at most 768 MiB of HBM per device.

v0:
```python
import jax
import jax.numpy as jnp
from jax import lax
from jax.sharding import PartitionSpec as P

EPSILON = 1e-6
ROPE_BASE = 10000.0


def rms_normed(values):
    return values * lax.rsqrt(jnp.mean(values * values, axis=-1, keepdims=True) + EPSILON)


def rotary(vectors, positions):
    half = vectors.shape[-1] // 2
    freqs = ROPE_BASE ** (-2.0 * jnp.arange(half, dtype=jnp.float32) / vectors.shape[-1])
    angle = positions[:, None, None] * freqs[None, None, :]
    cosine = jnp.cos(angle)
    sine = jnp.sin(angle)
    first = vectors[..., :half]
    second = vectors[..., half:]
    return jnp.concatenate([first * cosine - second * sine, second * cosine + first * sine], axis=-1)


def attend(hidden_blk, keys_blk, vals_blk, lens_blk, w_q, w_k, w_v, w_o):
    tok_count = hidden_blk.shape[0]
    seq_len, kv_heads, head_dim = keys_blk.shape[1], keys_blk.shape[2], keys_blk.shape[3]
    heads = w_q.shape[1] // head_dim
    group = heads // kv_heads
    hidden_f = hidden_blk.astype(jnp.float32)
    normed = rms_normed(hidden_f).astype(jnp.bfloat16)
    positions = lens_blk.astype(jnp.float32)
    query = rotary(jnp.dot(normed, w_q, preferred_element_type=jnp.float32).reshape(tok_count, heads, head_dim), positions)
    query = query.astype(jnp.bfloat16).reshape(tok_count, kv_heads, group, head_dim)
    key_new = rotary(jnp.dot(normed, w_k, preferred_element_type=jnp.float32).reshape(tok_count, kv_heads, head_dim), positions).astype(jnp.bfloat16)
    val_new = jnp.dot(normed, w_v, preferred_element_type=jnp.float32).astype(jnp.bfloat16).reshape(tok_count, kv_heads, head_dim)
    scale = head_dim ** -0.5
    scores = jnp.einsum("tkgd,tskd->tkgs", query, keys_blk, preferred_element_type=jnp.float32) * scale
    valid = jnp.arange(seq_len)[None, None, None, :] < lens_blk[:, None, None, None]
    scores = jnp.where(valid, scores, -jnp.inf)
    score_new = jnp.einsum("tkgd,tkd->tkg", query, key_new, preferred_element_type=jnp.float32) * scale
    peak = jnp.maximum(jnp.max(scores, axis=-1), score_new)
    weights = jnp.exp(scores - peak[..., None])
    weight_new = jnp.exp(score_new - peak)
    denominator = jnp.sum(weights, axis=-1) + weight_new
    mixed = jnp.einsum("tkgs,tskd->tkgd", weights.astype(jnp.bfloat16), vals_blk, preferred_element_type=jnp.float32)
    mixed = mixed + weight_new.astype(jnp.bfloat16).astype(jnp.float32)[..., None] * val_new.astype(jnp.float32)[:, :, None, :]
    attended = (mixed / denominator[..., None]).astype(jnp.bfloat16).reshape(tok_count, heads * head_dim)
    return (hidden_f + jnp.dot(attended, w_o, preferred_element_type=jnp.float32)).astype(jnp.bfloat16)


def skip_attend(hidden_blk, *rest):
    return jnp.zeros_like(hidden_blk)


def route(attn_out, ids_blk, w_r, n_experts, cap):
    mixed_in = rms_normed(attn_out.astype(jnp.float32)).astype(jnp.bfloat16)
    logits = jnp.dot(mixed_in.astype(jnp.float32), w_r, precision=lax.Precision.HIGHEST)
    gates = jax.nn.softmax(jnp.take_along_axis(logits, ids_blk, axis=1), axis=-1)
    flat_ids = ids_blk.reshape(-1)
    onehot = (flat_ids[:, None] == jnp.arange(n_experts)[None, :]).astype(jnp.int32)
    slot = jnp.sum(jnp.cumsum(onehot, axis=0) * onehot, axis=1) - 1
    target = (flat_ids * cap + slot).reshape(ids_blk.shape)
    placing = jnp.any(jnp.arange(n_experts * cap)[:, None, None] == target[None, :, :], axis=2).astype(jnp.bfloat16)
    outbound = jnp.dot(placing, mixed_in, preferred_element_type=jnp.float32).astype(jnp.bfloat16)
    return gates, target, outbound


def experts_apply(tokens, w_one, w_three, w_two):
    up_one = jnp.einsum("snci,nif->sncf", tokens, w_one, preferred_element_type=jnp.float32)
    up_three = jnp.einsum("snci,nif->sncf", tokens, w_three, preferred_element_type=jnp.float32)
    inner = (jax.nn.silu(up_one) * up_three).astype(jnp.bfloat16)
    return jnp.einsum("sncf,nfi->snci", inner, w_two, preferred_element_type=jnp.float32).astype(jnp.bfloat16)


def skip_experts(tokens, *rest):
    return jnp.zeros_like(tokens)


def combine(attn_out, gates, target, returned):
    rows = jnp.take(returned, target.reshape(-1), axis=0).reshape(target.shape[0], target.shape[1], returned.shape[1])
    mixed_sum = jnp.sum(gates[:, :, None] * rows.astype(jnp.float32), axis=1)
    return (attn_out.astype(jnp.float32) + mixed_sum).astype(jnp.bfloat16)


def solution(mesh):
    pool_size = mesh.shape["pool"]
    ep_size = mesh.shape["ep"]
    half = pool_size // 2
    n_att = half * ep_size

    def body(hidden, k_cache, v_cache, lengths, expert_ids, w_query, w_key, w_value, w_out, w_router, w_gate, w_up, w_down):
        row = lax.axis_index("pool")
        is_att = row < half
        sub = row % half
        tok_count = hidden.shape[0] // half
        model = hidden.shape[1]
        n_experts = w_router.shape[2]
        topk = expert_ids.shape[2]
        n_local = w_gate.shape[1] // half
        cap = max(2, (3 * tok_count * topk) // n_experts)
        start = sub * tok_count
        state = lax.dynamic_slice_in_dim(hidden, start, tok_count, 0)
        lens_blk = lax.dynamic_slice_in_dim(lengths, start, tok_count, 0)
        for layer in range(k_cache.shape[0]):
            keys_blk = lax.dynamic_slice_in_dim(k_cache[layer], start, tok_count, 0)
            vals_blk = lax.dynamic_slice_in_dim(v_cache[layer], start, tok_count, 0)
            ids_blk = lax.dynamic_slice_in_dim(expert_ids[layer], start, tok_count, 0)
            attended = lax.cond(is_att, attend, skip_attend, state, keys_blk, vals_blk, lens_blk, w_query[layer], w_key[layer], w_value[layer], w_out[layer])
            gates, target, outbound = route(attended, ids_blk, w_router[layer], n_experts, cap)
            grid = outbound.reshape(ep_size, half, n_local, cap, model).transpose(1, 0, 2, 3, 4)
            dispatch_buf = jnp.concatenate([jnp.zeros_like(grid), grid], axis=0).reshape(pool_size * ep_size, n_local, cap, model)
            arrived = lax.all_to_all(dispatch_buf, ("pool", "ep"), 0, 0, tiled=True)
            w_one = lax.dynamic_slice_in_dim(w_gate[layer], sub * n_local, n_local, 0)
            w_three = lax.dynamic_slice_in_dim(w_up[layer], sub * n_local, n_local, 0)
            w_two = lax.dynamic_slice_in_dim(w_down[layer], sub * n_local, n_local, 0)
            produced = lax.cond(is_att, skip_experts, experts_apply, arrived[:n_att], w_one, w_three, w_two)
            return_buf = jnp.concatenate([produced, jnp.zeros_like(produced)], axis=0)
            came_back = lax.all_to_all(return_buf, ("pool", "ep"), 0, 0, tiled=True)
            returned = came_back[n_att:].reshape(half, ep_size, n_local, cap, model).transpose(1, 0, 2, 3, 4).reshape(n_experts * cap, model)
            state = combine(attended, gates, target, returned)
        gathered = lax.all_gather(state, "pool", axis=0, tiled=True)
        return gathered[: half * tok_count]

    rows_spec = ("dp", "ep")
    in_specs = (P(rows_spec, None), P(None, rows_spec), P(None, rows_spec), P(rows_spec), P(None, rows_spec, None), P(), P(), P(), P(), P(), P(None, "ep"), P(None, "ep"), P(None, "ep"))
    return jax.shard_map(body, mesh=mesh, in_specs=in_specs, out_specs=P(rows_spec, None), check_vma=False)
```

profile of v0, /device:TPU:97, one launch (start us, length us, event | category | flops | bytes accessed | tf_op | source)
XLA Modules:
  0.0 1023.8 jit_solution(10809810408770239805)
XLA Ops:
  12.9 99.1 %conditional.4 = (f32[128,1536]{1,0:T(8,128)S(1)}, f32[128,1]{0,1:T(1,128)S(1)}) conditional(s32[]{:T(128)} %convert_element_type.228, () %tuple.56, (bf16[256,1536]{1,0:T(8,128)(2,1)}, s32[]{:T(128)}, s32[128]{0:T(128)}, bf16[2,1536,1536]{2,1,0:T(8,128)(2,1)}, bf16[2,256,128,2,128]{4,3,2,1,0:T(2,128)(2,1)}, ...), branch_computations={%region_0.1_spmd, %region_1.6_spmd} | conditional | flops 1518765312 | bytes 329170688 | solution.py:109
  14.1 12.7 %copy.119 = bf16[2,1536,1536]{1,2,0:T(8,128)(2,1)} copy(bf16[2,1536,1536]{2,1,0:T(8,128)(2,1)} %get-tuple-element.381) | data formatting | bytes 18874368 | tf_op jit(solution)/shard_map
  33.3 22.8 %copy.120 = bf16[2,256,128,2,128]{4,2,3,1,0:T(8,128)(2,1)} copy(bf16[2,256,128,2,128]{4,3,2,1,0:T(2,128)(2,1)} %get-tuple-element.382) | data formatting | bytes 67108864 | tf_op jit(solution)/shard_map
  56.2 5.8 slice-done
  61.9 5.5 fusion.170
  76.3 23.1 %copy.122 = bf16[2,256,128,2,128]{4,2,3,1,0:T(8,128)(2,1)} copy(bf16[2,256,128,2,128]{4,3,2,1,0:T(2,128)(2,1)} %get-tuple-element.384) | data formatting | bytes 67108864 | tf_op jit(solution)/shard_map
  99.5 5.8 slice-done.1
  105.4 2.4 fusion.31
  108.2 3.3 multiply_reduce_fusion
  113.5 2.5 copy.155
  116.1 7.0 concatenate.46.clone
  123.1 6.6 all-to-all-start
  129.7 117.4 %all-to-all-done = bf16[32,1,96,1536]{3,2,1,0:T(8,128)(2,1)} async-done(((bf16[32,1,96,1536]{3,2,1,0:T(8,128)(2,1)}), bf16[32,1,96,1536]{3,2,1,0:T(8,128)(2,1)}, u32[]{:S(2)}, u32[]{:S(2)}) %all-to-all-start) | async-done | bytes 9437216 | tf_op jit(solution)/shard_map/all_to_all | solution.py:113
  247.1 9.8 conditional.5
  254.2 2.7 broadcast.315
  256.9 7.0 concatenate.47
  263.9 94.0 %all-to-all-start.1 = ((bf16[32,1,96,1536]{3,2,1,0:T(8,128)(2,1)}), bf16[32,1,96,1536]{3,2,1,0:T(8,128)(2,1)}, u32[]{:S(2)}, u32[]{:S(2)}) async-start(bf16[32,1,96,1536]{3,2,1,0:T(8,128)(2,1)} %concatenate.47), calls=%async_computation.1 | async-start | bytes 18874368 | tf_op jit(solution)/shard_map/all_to_all | solution.py:119
  359.0 3.7 gather_fusion
  365.8 109.5 %all-to-all-done.1 = bf16[32,1,96,1536]{3,2,1,0:T(8,128)(2,1)} async-done(((bf16[32,1,96,1536]{3,2,1,0:T(8,128)(2,1)}), bf16[32,1,96,1536]{3,2,1,0:T(8,128)(2,1)}, u32[]{:S(2)}, u32[]{:S(2)}) %all-to-all-start.1) | async-done | bytes 9437216 | tf_op jit(solution)/shard_map/all_to_all | solution.py:119
  475.3 2.6 slice.231
  478.0 2.4 copy.133
  480.4 7.3 gather_fusion.1
  491.6 4.2 multiply_reduce_fusion.3
  497.0 92.2 %conditional.6 = (f32[128,1536]{1,0:T(8,128)S(1)}, f32[128,1]{0,1:T(1,128)S(1)}) conditional(s32[]{:T(128)} %convert_element_type.228, () %tuple.55, (bf16[128,1536]{1,0:T(8,128)(2,1)S(1)}, s32[128]{0:T(128)}, bf16[2,1536,1536]{2,1,0:T(8,128)(2,1)}, bf16[2,256,128,2,128]{4,3,2,1,0:T(2,128)(2,1)}, s32[]{:T(128)}, ...), branch_computations={%region_15.18_spmd, %region_16.23_spmd} | conditional | flops 1518765312 | bytes 319731840 | solution.py:109
  500.8 12.7 %copy.134 = bf16[2,1536,1536]{1,2,0:T(8,128)(2,1)} copy(bf16[2,1536,1536]{2,1,0:T(8,128)(2,1)} %get-tuple-element.394) | data formatting | bytes 18874368 | tf_op jit(solution)/shard_map
  513.5 2.3 slice-done.5
  519.5 22.8 %copy.135 = bf16[2,256,128,2,128]{4,2,3,1,0:T(8,128)(2,1)} copy(bf16[2,256,128,2,128]{4,3,2,1,0:T(2,128)(2,1)} %get-tuple-element.395) | data formatting | bytes 67108864 | tf_op jit(solution)/shard_map
  542.4 5.8 slice-done.2
  548.1 4.7 fusion.171
  554.4 22.8 %copy.137 = bf16[2,256,128,2,128]{4,2,3,1,0:T(8,128)(2,1)} copy(bf16[2,256,128,2,128]{4,3,2,1,0:T(2,128)(2,1)} %get-tuple-element.398) | data formatting | bytes 67108864 | tf_op jit(solution)/shard_map
  577.2 5.8 slice-done.3
  583.0 2.4 fusion.106
  585.7 3.2 multiply_reduce_fusion.1
  590.6 2.5 copy.156
  593.2 7.0 concatenate.48.clone
  600.2 14.1 %all-to-all-start.2 = ((bf16[32,1,96,1536]{3,2,1,0:T(8,128)(2,1)}), bf16[32,1,96,1536]{3,2,1,0:T(8,128)(2,1)}, u32[]{:S(2)}, u32[]{:S(2)}) async-start(bf16[32,1,96,1536]{3,2,1,0:T(8,128)(2,1)} %bitcast.313), calls=%async_computation.2 | async-start | bytes 18874368 | tf_op jit(solution)/shard_map/all_to_all | solution.py:113
  614.3 116.0 %all-to-all-done.2 = bf16[32,1,96,1536]{3,2,1,0:T(8,128)(2,1)} async-done(((bf16[32,1,96,1536]{3,2,1,0:T(8,128)(2,1)}), bf16[32,1,96,1536]{3,2,1,0:T(8,128)(2,1)}, u32[]{:S(2)}, u32[]{:S(2)}) %all-to-all-start.2) | async-done | bytes 9437216 | tf_op jit(solution)/shard_map/all_to_all | solution.py:113
  730.4 9.1 conditional.7
  736.8 2.7 broadcast.322
  739.5 7.0 concatenate.49
  746.5 95.4 %all-to-all-start.3 = ((bf16[32,1,96,1536]{3,2,1,0:T(8,128)(2,1)}), bf16[32,1,96,1536]{3,2,1,0:T(8,128)(2,1)}, u32[]{:S(2)}, u32[]{:S(2)}) async-start(bf16[32,1,96,1536]{3,2,1,0:T(8,128)(2,1)} %concatenate.49), calls=%async_computation.3 | async-start | bytes 18874368 | tf_op jit(solution)/shard_map/all_to_all | solution.py:119
  842.9 3.8 gather_fusion.2
  847.0 112.4 %all-to-all-done.3 = bf16[32,1,96,1536]{3,2,1,0:T(8,128)(2,1)} async-done(((bf16[32,1,96,1536]{3,2,1,0:T(8,128)(2,1)}), bf16[32,1,96,1536]{3,2,1,0:T(8,128)(2,1)}, u32[]{:S(2)}, u32[]{:S(2)}) %all-to-all-start.3) | async-done | bytes 9437216 | tf_op jit(solution)/shard_map/all_to_all | solution.py:119
  959.4 2.6 slice.233
  962.1 2.4 copy.148
  964.5 7.3 gather_fusion.3
  975.7 4.2 multiply_reduce_fusion.2
  981.9 32.6 %all-gather.2.cloned.1.call-done = bf16[512,1536]{1,0:T(8,128)(2,1)} async-done(((bf16[128,1536]{1,0:T(8,128)(2,1)}), bf16[512,1536]{1,0:T(8,128)(2,1)}) %all-gather.2.cloned.1.call-update) | async-done | bytes 1572880 | tf_op jit(solution)/shard_map/all_gather | solution.py:122
  (177 shorter events, 53.1 us)
Async XLA Ops:
  7.9 0.6 copy-start.16
  8.2 2.4 copy-start.14
  10.0 0.6 copy-start.18
  26.8 2.3 slice-start.4
  26.8 2.5 copy-start.6
  56.2 5.8 slice-start
  61.9 5.5 copy-start.4
  99.4 5.8 slice-start.1
  99.4 6.0 copy-start.5
  105.4 2.8 copy-start.7
  112.0 4.0 copy-start
  112.0 4.0 copy-start.26
  123.1 124.0 %all-to-all-start = ((bf16[32,1,96,1536]{3,2,1,0:T(8,128)(2,1)}), bf16[32,1,96,1536]{3,2,1,0:T(8,128)(2,1)}, u32[]{:S(2)}, u32[]{:S(2)}) async-start(bf16[32,1,96,1536]{3,2,1,0:T(8,128)(2,1)} %bitcast.312), calls=%async_computation | async-start | bytes 18874368 | tf_op jit(solution)/shard_map/all_to_all | solution.py:113
  263.9 94.0 %copy-start.10 = (s32[1,128,4]{1,2,0:T(4,128)S(1)}, s32[1,128,4]{1,2,0:T(4,128)}, u32[]{:S(2)}) copy-start(s32[1,128,4]{1,2,0:T(4,128)} %get-tuple-element.409) | copy-start | bytes 6148
  263.9 94.3 %copy-start.23 = (s32[128,4,1]{0,1,2:T(4,128)S(1)}, s32[128,4,1]{0,1,2:T(4,128)}, u32[]{:S(2)}) copy-start(s32[128,4,1]{0,1,2:T(4,128)} %get-tuple-element.444) | copy-start | bytes 6148
  263.9 94.6 %copy-start.1 = (f32[128,1536]{1,0:T(8,128)S(1)}, f32[128,1536]{1,0:T(8,128)}, u32[]{:S(2)}) copy-start(f32[128,1536]{1,0:T(8,128)} %copy-done) | copy-start | bytes 2359300
  263.9 94.6 %copy-start.8 = (f32[2,1536,16]{1,2,0:T(8,128)S(1)}, f32[2,1536,16]{1,2,0:T(8,128)}, u32[]{:S(2)}) copy-start(f32[2,1536,16]{1,2,0:T(8,128)} %param.34) | copy-start | bytes 589828
  263.9 94.6 %copy-start.27 = (f32[128]{0:T(128)S(1)}, f32[128]{0:T(128)}, u32[]{:S(2)}) copy-start(f32[128]{0:T(128)} %copy-done.26) | copy-start | bytes 1540
  263.9 211.4 %all-to-all-start.1 = ((bf16[32,1,96,1536]{3,2,1,0:T(8,128)(2,1)}), bf16[32,1,96,1536]{3,2,1,0:T(8,128)(2,1)}, u32[]{:S(2)}, u32[]{:S(2)}) async-start(bf16[32,1,96,1536]{3,2,1,0:T(8,128)(2,1)} %concatenate.47), calls=%async_computation.1 | async-start | bytes 18874368 | tf_op jit(solution)/shard_map/all_to_all | solution.py:119
  358.2 6.3 copy-start.12
  359.0 4.0 copy-start.17
  359.0 5.9 copy-start.15
  359.0 5.9 copy-start.19
  364.7 115.7 %copy-start.20 = (s32[512]{0:T(512)}, s32[512]{0:T(512)S(1)}, u32[]{:S(2)}) copy-start(s32[512]{0:T(512)S(1)} %fusion.159) | copy-start | bytes 6148
  513.5 2.3 slice-start.5
  542.4 5.8 slice-start.2
  548.1 5.8 copy-start.28
  577.2 5.8 slice-start.3
  589.2 4.0 copy-start.2
  589.2 4.0 copy-start.24
  600.2 130.1 %all-to-all-start.2 = ((bf16[32,1,96,1536]{3,2,1,0:T(8,128)(2,1)}), bf16[32,1,96,1536]{3,2,1,0:T(8,128)(2,1)}, u32[]{:S(2)}, u32[]{:S(2)}) async-start(bf16[32,1,96,1536]{3,2,1,0:T(8,128)(2,1)} %bitcast.313), calls=%async_computation.2 | async-start | bytes 18874368 | tf_op jit(solution)/shard_map/all_to_all | solution.py:113
  746.5 95.6 %copy-start.22 = (s32[128,4,1]{0,1,2:T(4,128)S(1)}, s32[128,4,1]{0,1,2:T(4,128)}, u32[]{:S(2)}) copy-start(s32[128,4,1]{0,1,2:T(4,128)} %get-tuple-element.408) | copy-start | bytes 6148
  746.5 95.8 %copy-start.13 = (s32[512]{0:T(512)S(1)}, s32[512]{0:T(512)}, u32[]{:S(2)}) copy-start(s32[512]{0:T(512)} %copy-done.12) | copy-start | bytes 6148
  746.5 95.8 %copy-start.21 = (s32[512]{0:T(512)S(1)}, s32[512]{0:T(512)}, u32[]{:S(2)}) copy-start(s32[512]{0:T(512)} %copy-done.20) | copy-start | bytes 6148
  746.5 95.8 %copy-start.3 = (f32[128,1536]{1,0:T(8,128)S(1)}, f32[128,1536]{1,0:T(8,128)}, u32[]{:S(2)}) copy-start(f32[128,1536]{1,0:T(8,128)} %copy-done.2) | copy-start | bytes 2359300
  746.5 95.8 %copy-start.9 = (f32[2,1536,16]{1,2,0:T(8,128)S(1)}, f32[2,1536,16]{1,2,0:T(8,128)}, u32[]{:S(2)}) copy-start(f32[2,1536,16]{1,2,0:T(8,128)} %param.34) | copy-start | bytes 589828
  746.5 95.8 %copy-start.25 = (f32[128]{0:T(128)S(1)}, f32[128]{0:T(128)}, u32[]{:S(2)}) copy-start(f32[128]{0:T(128)} %copy-done.24) | copy-start | bytes 1540
  746.5 212.9 %all-to-all-start.3 = ((bf16[32,1,96,1536]{3,2,1,0:T(8,128)(2,1)}), bf16[32,1,96,1536]{3,2,1,0:T(8,128)(2,1)}, u32[]{:S(2)}, u32[]{:S(2)}) async-start(bf16[32,1,96,1536]{3,2,1,0:T(8,128)(2,1)} %concatenate.49), calls=%async_computation.3 | async-start | bytes 18874368 | tf_op jit(solution)/shard_map/all_to_all | solution.py:119
  842.0 172.5 %all-gather.2.cloned.1.call-start = ((), (), s32[]{:S(2)}) async-start(), calls=%async_computation.4 | async-start | bytes 1966080 | tf_op jit(solution)/shard_map/all_gather | solution.py:122
  842.9 3.9 copy-start.11
Sparse Core Ops, SparseCore 0:
  982.0 32.4 all-gather.1
where the time goes:
time: 1030 us; the launch traced here: 1020 us
  waiting for transfers between devices  488 us (47%)
  local copies, waits for them, and re-layouts  235 us (23%)
  starting transfers between devices  210 us (20%)
  matrix products  33.2 us (3%)
  other arithmetic  27.9 us (3%)
  loops' own time  15 us (1%)
  between operations  14.4 us (1%)
    all_to_all x2, waiting for transfers between devices, body(): arrived = lax.all_to_all(dispatch_buf, ('pool', 'ep'), 0, 0, tiled=True)  233 us
    all_to_all x2, waiting for transfers between devices, body(): came_back = lax.all_to_all(return_buf, ('pool', 'ep'), 0, 0, tiled=True)  222 us
    all_to_all x2, starting transfers between devices, body(): came_back = lax.all_to_all(return_buf, ('pool', 'ep'), 0, 0, tiled=True)  189 us
    another operation x13, local copies, waits for them, and re-layouts  126 us
    all_gather x1, waiting for transfers between devices, body(): gathered = lax.all_gather(state, 'pool', axis=0, tiled=True)  32.6 us
    all_to_all x2, starting transfers between devices, body(): arrived = lax.all_to_all(dispatch_buf, ('pool', 'ep'), 0, 0, tiled=True)  20.7 us
  transfers between devices with their start and end apart: 5, of which 5 were waited for; matrix products, arithmetic and copies ran while one was open for 1% of the time, Pallas kernels for 0%

commit v1 on v0

v1 whole, which is shorter than its diff:
```python
import functools

import jax
import jax.numpy as jnp
from jax import lax
from jax.experimental import pallas as pl
from jax.experimental.pallas import tpu as pltpu
from jax.sharding import PartitionSpec as P

EPSILON = 1e-6
ROPE_BASE = 10000.0
MESH = pl.DeviceIdType.MESH
F32 = jnp.float32
BF16 = jnp.bfloat16
CORES = 2
HP = 16
LANES = 128
NW = 384
NS = 512
R13 = 3


def step_kernel(cfg, x_hbm, kc_hbm, vc_hbm, len_ref, ids_ref, wq_hbm, wk_hbm, wv_hbm, wo_hbm, wr_ref, wg_hbm, wu_hbm, wd_hbm,
                out_hbm,
                xin, xs, a_scr, q_scr, kn_scr, vn_scr, mn_scr, den_scr, s_scr, p_scr, cos_scr, sin_scr, wr3,
                kbuf, vbuf, wqb, wkb, wvb, wob, w13, w2b,
                u_all, g_all, gcol, inner, psum, pairbuf, rbuf, fin,
                sem_x, sem_w, sem_k, sem_v, sem_g, sem_u, sem_d,
                du_s, du_r, dg_s, dg_r, pr_s, pr_r, rr_s, rr_r, fs, fr, sem_o):
    layers, tok, model, heads, kvh, hd, seq, ff, nloc, nx, npool, nexp, topk = cfg
    ep = nx * CORES
    rows = ep * tok
    half = tok // 2
    group = heads // kvh
    pool = lax.axis_index("pool")
    e = lax.axis_index("ep")
    xx = lax.div(e, CORES)
    c = lax.rem(e, CORES)
    oc = 1 - c
    xr = lax.rem(xx + 1, nx)
    xl = lax.rem(xx + nx - 1, nx)
    xf = lax.rem(xx + 2, nx)
    partner = xx * CORES + oc
    er = xr * CORES + c
    el = xl * CORES + c
    ef = xf * CORES + c
    pn = lax.rem(pool + 1, npool)
    pp = lax.rem(pool + npool - 1, npool)
    pf = lax.rem(pool + 2, npool)

    def to_ep(i):
        return {"ep": i}

    def to_pool(i):
        return {"pool": i}

    barrier = pltpu.get_barrier_semaphore()
    for dev in (to_ep(partner), to_ep(er), to_ep(el), to_pool(pn), to_pool(pp)):
        pl.semaphore_signal(barrier, inc=1, device_id=dev, device_id_type=MESH)

    kpieces = sem_k.shape[0]
    kp = tok // kpieces
    tok0 = pl.multiple_of(pool * tok, tok)

    def k_copy(l, i):
        return pltpu.make_async_copy(kc_hbm.at[l, pl.ds(tok0 + i * kp, kp)], kbuf.at[pl.ds(i * kp, kp)], sem_k.at[i])

    def v_copy(l, i):
        return pltpu.make_async_copy(vc_hbm.at[l, pl.ds(tok0 + i * kp, kp)], vbuf.at[pl.ds(i * kp, kp)], sem_v.at[i])

    def w_copy(l, i):
        src = (wq_hbm, wk_hbm, wv_hbm, wo_hbm)[i]
        dst = (wqb, wkb, wvb, wob)[i]
        return pltpu.make_async_copy(src.at[l], dst, sem_w.at[i])

    n13 = ff // NW
    n2 = model // NS
    tot13 = layers * nloc * n13
    tot2 = layers * nloc * n2

    def g_copies(t):
        li = lax.div(t, n13)
        j = lax.rem(t, n13)
        l = lax.div(li, nloc)
        i = lax.rem(li, nloc)
        slot = lax.rem(t, R13)
        cols = pl.ds(pl.multiple_of(j * NW, NW), NW)
        return (pltpu.make_async_copy(wg_hbm.at[l, i, :, cols], w13.at[slot, :, pl.ds(0, NW)], sem_g.at[slot]),
                pltpu.make_async_copy(wu_hbm.at[l, i, :, cols], w13.at[slot, :, pl.ds(NW, NW)], sem_u.at[slot]))

    def d_copy(t):
        li = lax.div(t, n2)
        j = lax.rem(t, n2)
        l = lax.div(li, nloc)
        i = lax.rem(li, nloc)
        cols = pl.ds(pl.multiple_of(j * NS, NS), NS)
        return pltpu.make_async_copy(wd_hbm.at[l, i, :, cols], w2b.at[j], sem_d.at[j])

    x_copy = pltpu.make_async_copy(x_hbm.at[pl.ds(tok0, tok)], xin, sem_x.at[0])
    x_copy.start()
    for i in range(3):
        w_copy(0, i).start()
    for i in range(kpieces):
        k_copy(0, i).start()

    lane = lax.broadcasted_iota(jnp.int32, (tok, hd), 1)
    pos_i = jnp.zeros((tok, hd), jnp.int32)
    row_i = lax.broadcasted_iota(jnp.int32, (tok, hd), 0)
    for t in range(tok):
        pos_i = jnp.where(row_i == t, len_ref[pool * tok + t], pos_i)
    half_hd = hd // 2
    pair = jnp.where(lane < half_hd, lane, lane - half_hd).astype(F32)
    freqs = jnp.exp(pair * (-2.0 / hd) * jnp.log(jnp.full((tok, hd), ROPE_BASE, F32)))
    angle = pos_i.astype(F32) * freqs
    cos_scr[...] = jnp.cos(angle)
    sn = jnp.sin(angle)
    sin_scr[...] = jnp.where(lane < half_hd, -sn, sn)
    for l in range(layers):
        w = wr_ref[l]
        hi = w.astype(BF16)
        r1 = w - hi.astype(F32)
        mid = r1.astype(BF16)
        lo = (r1 - mid.astype(F32)).astype(BF16)
        wr3[l, pl.ds(0, nexp), :] = hi
        wr3[l, pl.ds(nexp, nexp), :] = mid
        wr3[l, pl.ds(2 * nexp, nexp), :] = lo
    zero_rows = jnp.zeros((tok, hd), F32)
    for h in range(heads, HP):
        q_scr[pl.ds(h, tok, stride=HP), :] = zero_rows
        kn_scr[pl.ds(h, tok, stride=HP), :] = zero_rows
        vn_scr[pl.ds(h, tok, stride=HP), :] = zero_rows

    pl.semaphore_wait(barrier, 5)
    x_copy.wait()
    xs[...] = xin[...].astype(F32)

    scale = hd ** -0.5
    rix = lax.broadcasted_iota(jnp.int32, (HP, seq * kvh), 0)
    cix = lax.broadcasted_iota(jnp.int32, (HP, seq * kvh), 1)
    own_kv = lax.rem(cix, kvh) == lax.div(rix, group)
    colpos = jnp.where(own_kv, lax.div(cix, kvh), 2 * seq)

    def rotate(v):
        return v * cos_scr[...] + pltpu.roll(v, half_hd, 1) * sin_scr[...]

    def attention(l):
        xf32 = xs[...]
        h = (xf32 * lax.rsqrt(jnp.mean(xf32 * xf32, axis=-1, keepdims=True) + EPSILON)).astype(BF16)
        w_copy(l, 0).wait()
        per = 256 // hd
        for n in range(heads // per):
            qn = jnp.dot(h, wqb[:, n * 256:(n + 1) * 256], preferred_element_type=F32)
            for s in range(per):
                r = rotate(qn[:, s * hd:(s + 1) * hd]).astype(BF16).astype(F32)
                q_scr[pl.ds(n * per + s, tok, stride=HP), :] = r
        w_copy(l, 1).wait()
        kn = jnp.dot(h, wkb[...], preferred_element_type=F32)
        w_copy(l, 2).wait()
        vn = jnp.dot(h, wvb[...], preferred_element_type=F32)
        for kv in range(kvh):
            r = rotate(kn[:, kv * hd:(kv + 1) * hd]).astype(BF16).astype(F32)
            v = vn[:, kv * hd:(kv + 1) * hd].astype(BF16).astype(F32)
            for g in range(group):
                kn_scr[pl.ds(kv * group + g, tok, stride=HP), :] = r
                vn_scr[pl.ds(kv * group + g, tok, stride=HP), :] = v
        if l == 0:
            for i in range(kpieces):
                v_copy(l, i).start()
            w_copy(l, 3).start()

        def qk(i, carry):
            k_copy(l, i).wait()
            for s in range(kp):
                t = i * kp + s
                r16 = pl.ds(pl.multiple_of(t * HP, HP), HP)
                q = q_scr[r16, :].astype(BF16)
                sc = lax.dot_general(q, kbuf[t], (((1,), (1,)), ((), ())), preferred_element_type=F32)
                s_scr[r16, :] = jnp.where(colpos < len_ref[pool * tok + t], sc * scale, -jnp.inf)
            return carry

        lax.fori_loop(0, kpieces, qk, 0)
        if l == 0:
            for t in range(R13):
                for cp in g_copies(t):
                    cp.start()

        def soft(i, carry):
            rr = pl.ds(pl.multiple_of(i * 128, 128), 128)
            sc = s_scr[rr, :]
            s_new = jnp.sum(q_scr[rr, :] * kn_scr[rr, :], axis=-1, keepdims=True) * scale
            peak = jnp.maximum(jnp.max(sc, axis=-1, keepdims=True), s_new)
            wts = jnp.exp(sc - peak)
            w_new = jnp.exp(s_new - peak)
            den = jnp.sum(wts, axis=-1, keepdims=True) + w_new
            p_scr[rr, :] = wts.astype(BF16)
            mn_scr[rr, :] = w_new.astype(BF16).astype(F32) * vn_scr[rr, :]
            den_scr[rr, :] = jnp.broadcast_to(den, (128, hd))
            return carry

        lax.fori_loop(0, tok * HP // 128, soft, 0)

        def pv(i, carry):
            v_copy(l, i).wait()
            for s in range(kp):
                t = i * kp + s
                r16 = pl.ds(pl.multiple_of(t * HP, HP), HP)
                m = jnp.dot(p_scr[r16, :], vbuf[t], preferred_element_type=F32)
                mn_scr[r16, :] = ((m + mn_scr[r16, :]) / den_scr[r16, :]).astype(BF16).astype(F32)
            return carry

        lax.fori_loop(0, kpieces, pv, 0)
        att = jnp.concatenate([mn_scr[pl.ds(h, tok, stride=HP), :].astype(BF16) for h in range(heads)], axis=1)
        w_copy(l, 3).wait()
        for n in range(model // 256):
            cs = slice(n * 256, (n + 1) * 256)
            a_scr[:, cs] = (xs[:, cs] + jnp.dot(att, wob[:, cs], preferred_element_type=F32)).astype(BF16).astype(F32)
        a = a_scr[...]
        u = (a * lax.rsqrt(jnp.mean(a * a, axis=-1, keepdims=True) + EPSILON)).astype(BF16)
        u_all[pl.ds(pl.multiple_of(e * tok, tok), tok), :] = u
        parts = lax.dot_general(wr3[l], u, (((1,), (1,)), ((), ())), preferred_element_type=F32)
        logits = (parts[2 * nexp:3 * nexp] + parts[nexp:2 * nexp]) + parts[0:nexp]
        ids = ids_ref[l]
        mine = ids[:, 0:tok]
        for i in range(1, npool):
            mine = jnp.where(pool == i, ids[:, i * tok:(i + 1) * tok], mine)
        eix = lax.broadcasted_iota(jnp.int32, (nexp, tok), 0)
        hit = eix == mine[0:1, :]
        for k in range(1, topk):
            hit = jnp.logical_or(hit, eix == mine[k:k + 1, :])
        ml = jnp.where(hit, logits, -jnp.inf)
        ex = jnp.exp(ml - jnp.max(ml, axis=0, keepdims=True))
        gates = ex / jnp.sum(ex, axis=0, keepdims=True)
        g_all[e] = jnp.concatenate([gates, jnp.zeros((nexp, LANES - tok), F32)], axis=1)

    def blk(i):
        return pl.ds(pl.multiple_of(i * tok, tok), tok)

    def hblk(i, s):
        return pl.ds(pl.multiple_of(i * tok + s * half, half), half)

    def dcopy(i, dev, rws, gix):
        a = pltpu.make_async_remote_copy(src_ref=u_all.at[rws], dst_ref=u_all.at[rws], send_sem=du_s.at[i], recv_sem=du_r.at[i],
                                         device_id=dev, device_id_type=MESH)
        if gix is None:
            return (a,)
        b = pltpu.make_async_remote_copy(src_ref=g_all.at[gix], dst_ref=g_all.at[gix], send_sem=dg_s.at[i], recv_sem=dg_r.at[i],
                                         device_id=dev, device_id_type=MESH)
        return (a, b)

    def start(cs):
        for cp in cs:
            cp.start()

    def wait_recv(cs):
        for cp in cs:
            cp.wait_recv()

    def wait_send(cs):
        for cp in cs:
            cp.wait_send()

    def dispatch():
        t1 = dcopy(1, to_ep(er), blk(e), e)
        t2 = dcopy(2, to_ep(el), blk(e), e)
        t0 = dcopy(0, to_ep(partner), blk(e), e)
        start(t1)
        start(t2)
        start(t0)
        wait_recv(t1)
        t3 = dcopy(3, to_ep(er), hblk(el, 0), el)
        start(t3)
        t5 = dcopy(5, to_ep(partner), blk(el), el)
        start(t5)
        wait_recv(t2)
        t4 = dcopy(4, to_ep(el), hblk(er, 1), None)
        start(t4)
        t6 = dcopy(6, to_ep(partner), blk(er), er)
        start(t6)
        wait_recv(t3)
        wait_recv(t4)
        t7 = dcopy(7, to_ep(partner), blk(ef), ef)
        start(t7)
        for t in (t0, t5, t6, t7):
            wait_recv(t)
        return (t0, t1, t2, t3, t4, t5, t6, t7)

    def gate_columns():
        gt = jnp.transpose(g_all[...].reshape(ep * nexp, LANES))
        gt = gt[0:tok, :]
        lix = lax.broadcasted_iota(jnp.int32, (tok, ep * nexp), 1)
        for i in range(nloc):
            for b in range(ep):
                col = jnp.sum(jnp.where(lix == b * nexp + e * nloc + i, gt, 0.0), axis=1, keepdims=True)
                gcol[i, pl.ds(b * tok, tok), :] = jnp.broadcast_to(col, (tok, LANES))

    def experts(l, i):
        base13 = (l * nloc + i) * n13
        base2 = (l * nloc + i) * n2

        def up(j, carry):
            t = base13 + j
            slot = lax.rem(t, R13)
            for cp in g_copies(t):
                cp.wait()
            hh = jnp.dot(u_all[...], w13[slot], preferred_element_type=F32)
            gate = hh[:, 0:NW]
            act = gate * jax.nn.sigmoid(gate) * hh[:, NW:2 * NW]
            inner[:, pl.ds(pl.multiple_of(j * NW, NW), NW)] = act.astype(BF16)

            @pl.when(t + R13 < tot13)
            def _():
                for cp in g_copies(t + R13):
                    cp.start()
            return carry

        lax.fori_loop(0, n13, up, 0)

        def down(j, carry):
            t = base2 + j
            d_copy(t).wait()
            y = jnp.dot(inner[...], w2b[j], preferred_element_type=F32).astype(BF16).astype(F32)
            gc = gcol[i]
            for s in range(NS // LANES):
                ys = y[:, s * LANES:(s + 1) * LANES]
                term = jnp.where(gc > 0.0, gc * ys, 0.0)
                cols = pl.ds(pl.multiple_of(j * NS + s * LANES, LANES), LANES)
                if i == 0:
                    psum[:, cols] = term
                else:
                    psum[:, cols] = psum[:, cols] + term

            @pl.when(t + n2 < tot2)
            def _():
                d_copy(t + n2).start()
            return carry

        lax.fori_loop(0, n2, down, 0)

    def rcopy(i, dev, rws):
        return pltpu.make_async_remote_copy(src_ref=psum.at[rws], dst_ref=rbuf.at[i], send_sem=rr_s.at[i], recv_sem=rr_r.at[i],
                                            device_id=dev, device_id_type=MESH)

    def give_back():
        order = (xf, xr, xl, xx)
        pairs = []
        for k in range(nx):
            cp = pltpu.make_async_remote_copy(src_ref=psum.at[blk(order[k] * CORES + oc)], dst_ref=pairbuf.at[k], send_sem=pr_s.at[k],
                                              recv_sem=pr_r.at[k], device_id=to_ep(partner), device_id_type=MESH)
            cp.start()
            pairs.append(cp)

        def add_pair(k):
            pairs[k].wait_recv()
            rws = blk(order[k] * CORES + c)
            psum[rws, :] = psum[rws, :] + pairbuf[k]

        m0 = rcopy(0, to_ep(er), hblk(ef, 1))
        m1 = rcopy(1, to_ep(el), hblk(ef, 0))
        m2 = rcopy(2, to_ep(er), hblk(er, 0))
        m3 = rcopy(3, to_ep(el), hblk(el, 1))
        m4 = rcopy(4, to_ep(er), hblk(er, 1))
        m5 = rcopy(5, to_ep(el), hblk(el, 0))
        add_pair(0)
        m0.start()
        m1.start()
        add_pair(1)
        m2.start()
        add_pair(2)
        m3.start()
        m0.wait_recv()
        psum[hblk(er, 1), :] = psum[hblk(er, 1), :] + rbuf[0]
        m4.start()
        m1.wait_recv()
        psum[hblk(el, 0), :] = psum[hblk(el, 0), :] + rbuf[1]
        m5.start()
        add_pair(3)
        m2.wait_recv()
        psum[hblk(e, 0), :] = psum[hblk(e, 0), :] + rbuf[2]
        m3.wait_recv()
        psum[hblk(e, 1), :] = psum[hblk(e, 1), :] + rbuf[3]
        m5.wait_recv()
        xs[0:half, :] = (a_scr[0:half, :] + (psum[hblk(e, 0), :] + rbuf[5])).astype(BF16).astype(F32)
        m4.wait_recv()
        xs[half:tok, :] = (a_scr[half:tok, :] + (psum[hblk(e, 1), :] + rbuf[4])).astype(BF16).astype(F32)
        wait_send(pairs)
        wait_send((m0, m1, m2, m3, m4, m5))

    for l in range(layers):
        attention(l)
        sent = dispatch()
        gate_columns()
        if l == 0:
            for t in range(n2):
                d_copy(t).start()
        for i in range(nloc):
            experts(l, i)
            if i == 0 and l + 1 < layers:
                for k in range(4):
                    w_copy(l + 1, k).start()
                for k in range(kpieces):
                    k_copy(l + 1, k).start()
                    v_copy(l + 1, k).start()
        for s in sent:
            wait_send(s)
        give_back()

    def fcopy(i, dev, rws):
        return pltpu.make_async_remote_copy(src_ref=fin.at[rws], dst_ref=fin.at[rws], send_sem=fs.at[i], recv_sem=fr.at[i],
                                            device_id=dev, device_id_type=MESH)

    def ocopy(i):
        return pltpu.make_async_copy(fin.at[blk(i)], out_hbm.at[blk(i)], sem_o.at[i])

    fin[blk(pool), :] = xs[...].astype(BF16)
    f0 = fcopy(0, to_pool(pn), blk(pool))
    f1 = fcopy(1, to_pool(pp), blk(pool))
    f0.start()
    f1.start()
    ocopy(pool).start()
    f0.wait_recv()
    f2 = fcopy(2, to_pool(pn), hblk(pp, 0))
    f2.start()
    ocopy(pp).start()
    f1.wait_recv()
    f3 = fcopy(3, to_pool(pp), hblk(pn, 1))
    f3.start()
    ocopy(pn).start()
    f2.wait_recv()
    f3.wait_recv()
    ocopy(pf).start()
    for i in (pool, pp, pn, pf):
        ocopy(i).wait()
    wait_send((f0, f1, f2, f3))


def solution(mesh):
    npool = mesh.shape["pool"]
    ep = mesh.shape["ep"]
    nx = ep // CORES

    def body(hidden, k_cache, v_cache, lengths, expert_ids, w_query, w_key, w_value, w_out, w_router, w_gate, w_up, w_down):
        layers, local, seq, kvh, hd = k_cache.shape
        model = hidden.shape[1]
        tok = local // npool
        heads = w_query.shape[2] // hd
        nloc, _, ff = w_gate.shape[1:]
        nexp = w_router.shape[2]
        topk = expert_ids.shape[2]
        kc = k_cache.reshape(layers, local, seq * kvh, hd)
        vc = v_cache.reshape(layers, local, seq * kvh, hd)
        ids_t = expert_ids.transpose(0, 2, 1)
        wr_t = w_router.transpose(0, 2, 1)
        cfg = (layers, tok, model, heads, kvh, hd, seq, ff, nloc, nx, npool, nexp, topk)
        rows = ep * tok
        half = tok // 2
        hbm = pl.BlockSpec(memory_space=pl.ANY)
        vmem = pl.BlockSpec(memory_space=pltpu.VMEM)
        smem = pl.BlockSpec(memory_space=pltpu.SMEM)
        kpieces = 8
        dma = pltpu.SemaphoreType.DMA
        n2 = model // NS
        scratch = [
            pltpu.VMEM((tok, model), BF16), pltpu.VMEM((tok, model), F32), pltpu.VMEM((tok, model), F32),
            pltpu.VMEM((tok * HP, hd), F32), pltpu.VMEM((tok * HP, hd), F32), pltpu.VMEM((tok * HP, hd), F32),
            pltpu.VMEM((tok * HP, hd), F32), pltpu.VMEM((tok * HP, hd), F32),
            pltpu.VMEM((tok * HP, seq * kvh), F32), pltpu.VMEM((tok * HP, seq * kvh), BF16),
            pltpu.VMEM((tok, hd), F32), pltpu.VMEM((tok, hd), F32), pltpu.VMEM((layers, 3 * nexp, model), BF16),
            pltpu.VMEM((tok, seq * kvh, hd), BF16), pltpu.VMEM((tok, seq * kvh, hd), BF16),
            pltpu.VMEM((model, heads * hd), BF16), pltpu.VMEM((model, kvh * hd), BF16), pltpu.VMEM((model, kvh * hd), BF16),
            pltpu.VMEM((heads * hd, model), BF16),
            pltpu.VMEM((R13, model, 2 * NW), BF16), pltpu.VMEM((n2, ff, NS), BF16),
            pltpu.VMEM((rows, model), BF16), pltpu.VMEM((ep, nexp, LANES), F32), pltpu.VMEM((nloc, rows, LANES), F32),
            pltpu.VMEM((rows, ff), BF16), pltpu.VMEM((rows, model), F32), pltpu.VMEM((nx, tok, model), F32),
            pltpu.VMEM((6, half, model), F32), pltpu.VMEM((local, model), BF16),
            dma((1,)), dma((4,)), dma((kpieces,)), dma((kpieces,)), dma((R13,)), dma((R13,)), dma((n2,)),
            dma((8,)), dma((8,)), dma((8,)), dma((8,)), dma((nx,)), dma((nx,)), dma((6,)), dma((6,)), dma((4,)), dma((4,)),
            dma((npool,)),
        ]
        call = pl.pallas_call(
            functools.partial(step_kernel, cfg),
            out_shape=jax.ShapeDtypeStruct((local, model), BF16),
            in_specs=[hbm, hbm, hbm, smem, vmem, hbm, hbm, hbm, hbm, vmem, hbm, hbm, hbm],
            out_specs=hbm,
            scratch_shapes=scratch,
            compiler_params=pltpu.CompilerParams(collective_id=0, has_side_effects=True, vmem_limit_bytes=66_000_000),
        )
        return call(hidden, kc, vc, lengths, ids_t, w_query, w_key, w_value, w_out, wr_t, w_gate, w_up, w_down)

    rows_spec = ("dp", "ep")
    in_specs = (P(rows_spec, None), P(None, rows_spec), P(None, rows_spec), P(rows_spec), P(None, rows_spec, None), P(), P(), P(), P(), P(), P(None, "ep"), P(None, "ep"), P(None, "ep"))
    return jax.shard_map(body, mesh=mesh, in_specs=in_specs, out_specs=P(rows_spec, None), check_vma=False)
```

time: 1030 us -> 158 us (0.15)
  waiting for transfers between devices: 488 us -> 0 us
  local copies, waits for them, and re-layouts: 235 us -> 2.06 us
  starting transfers between devices: 210 us -> 0 us
  Pallas kernels: 0 us -> 154 us
  matrix products: 33.2 us -> 0 us
  other arithmetic: 27.9 us -> 0 us
  loops' own time: 15 us -> 0 us
  between operations: 14.4 us -> 0.01 us
    all_to_all x4 -> x0, waiting for transfers between devices: 455 us -> none  [the longest x2 233 us: body(): arrived = lax.all_to_all(dispatch_buf, ('pool', 'ep'), 0, 0, tiled=True)]
    all_to_all x4 -> x0, starting transfers between devices: 210 us -> none  [the longest x2 189 us: body(): came_back = lax.all_to_all(return_buf, ('pool', 'ep'), 0, 0, tiled=True)]
    pallas_call x0 -> x1, Pallas kernels: none -> 154 us  [body(): call(hidden, kc, vc, lengths, ids_t, w_query, w_key, w_value, w_out, wr_t...]
    another operation x13 -> x0, local copies, waits for them, and re-layouts: 126 us -> none
    slice x19 -> x0, local copies, waits for them, and re-layouts: 37.2 us -> none  [the longest x4 11.5 us: body(): keys_blk = lax.dynamic_slice_in_dim(k_cache[layer], start, tok_count, 0)]
    dot_general x18 -> x0, matrix products: 33.2 us -> none  [the longest x2 10.3 us: attend(): jnp.einsum('tkgd,tskd->tkgs', query, keys_blk, preferred_element_type=jnp...]
    all_gather x1 -> x0, waiting for transfers between devices: 32.6 us -> none  [body(): gathered = lax.all_gather(state, 'pool', axis=0, tiled=True)]
    concatenate x10 -> x0, local copies, waits for them, and re-layouts: 30.1 us -> none  [the longest x2 14.1 us: body(): jnp.concatenate([jnp.zeros_like(grid), grid], axis=0)]
  transfers between devices with their start and end apart: 5 -> 0, of which waited for: 5 -> 0; matrix products, arithmetic and copies ran while one was open for 1% -> 0% of each run, Pallas kernels for 0% -> 0%
where the time goes in v1:
time: 158 us; the launch traced here: 157 us
  Pallas kernels  154 us (97%)
  local copies, waits for them, and re-layouts  2.06 us (1%)
    pallas_call x1, Pallas kernels, body(): call(hidden, kc, vc, lengths, ids_t, w_query, w_key, w_value, w_out, wr_t...  154 us

profile of v1, /device:TPU:97, one launch (start us, length us, event | category | flops | bytes accessed | tf_op | source)
XLA Modules:
  0.0 156.5 jit_solution(2847700030753043501)
XLA Ops:
  0.0 154.4 %shard_map.127 = bf16[256,1536]{1,0:T(8,128)(2,1)} custom-call(bf16[256,1536]{1,0:T(8,128)(2,1)} %x_hbm.1, bf16[2,256,256,128]{3,2,1,0:T(8,128)(2,1)} %bitcast.4, bf16[2,256,256,128]{3,2,1,0:T(8,128)(2,1)} %bitcast.5, s32[256]{0:T(256)} %len_ref.1, s32[2,4,256]{2,1,0:T(4,128)} %bitcast.7, bf16[2,1536,1536]{2,1,0:T(8,128)(2,1)} %wq_hbm.1, ...), custom_call_target="tpu_custom_call" | custom-call | tf_op jit(solution)/shard_map/pallas_call | solution.py:487
  154.4 2.1 %copy.15 = bf16[256,1536]{1,0:T(8,128)(2,1)} copy(bf16[256,1536]{1,0:T(8,128)(2,1)} %shard_map.127) | data formatting | bytes 1572864

commit v2 on v1

v2 whole, which is shorter than its diff:
```python
import functools

import jax
import jax.numpy as jnp
from jax import lax
from jax.experimental import pallas as pl
from jax.experimental.pallas import tpu as pltpu
from jax.sharding import PartitionSpec as P

EPSILON = 1e-6
ROPE_BASE = 10000.0
MESH = pl.DeviceIdType.MESH
F32 = jnp.float32
BF16 = jnp.bfloat16
CORES = 2
HP = 16
LANES = 128
NW = 384
R13 = 4
HALVES = 2


def step_kernel(cfg, x_hbm, kc_hbm, vc_hbm, len_ref, ids_ref, wq_hbm, wk_hbm, wv_hbm, wo_hbm, wr_ref, wg_hbm, wu_hbm, wd_hbm,
                out_hbm,
                xin, xs, a_scr, q_scr, kn_scr, vn_scr, mn_scr, den_scr, s_scr, p_scr, cos_scr, sin_scr, wr3,
                kbuf, vbuf, wqb, wkb, wvb, wob, w13, w2b,
                u_all, g_all, gcol, inner, psum, pairbuf, rbuf, fin,
                sem_x, sem_w, sem_k, sem_v, sem_g, sem_u, sem_d,
                du_s, du_r, dg_s, dg_r, pr_s, pr_r, rr_s, rr_r, fs, fr, sem_o):
    layers, tok, model, heads, kvh, hd, seq, ff, nloc, nx, npool, nexp, topk = cfg
    ep = nx * CORES
    rows = ep * tok
    ht = tok // HALVES
    hrows = rows // HALVES
    half = ht // 2
    group = heads // kvh
    pool = lax.axis_index("pool")
    e = lax.axis_index("ep")
    xx = lax.div(e, CORES)
    c = lax.rem(e, CORES)
    oc = 1 - c
    xr = lax.rem(xx + 1, nx)
    xl = lax.rem(xx + nx - 1, nx)
    xf = lax.rem(xx + 2, nx)
    partner = xx * CORES + oc
    dr = xr * CORES + oc
    dl = xl * CORES + oc
    er = xr * CORES + c
    el = xl * CORES + c
    ef = xf * CORES + c
    pn = lax.rem(pool + 1, npool)
    pp = lax.rem(pool + npool - 1, npool)
    pf = lax.rem(pool + 2, npool)

    def to_ep(i):
        return {"ep": i}

    def to_pool(i):
        return {"pool": i}

    barrier = pltpu.get_barrier_semaphore()
    for dev in (to_ep(partner), to_ep(er), to_ep(el), to_ep(dr), to_ep(dl), to_pool(pn), to_pool(pp)):
        pl.semaphore_signal(barrier, inc=1, device_id=dev, device_id_type=MESH)

    kpieces = sem_k.shape[0]
    kp = tok // kpieces
    tok0 = pl.multiple_of(pool * tok, tok)

    def k_copy(l, i):
        return pltpu.make_async_copy(kc_hbm.at[l, pl.ds(tok0 + i * kp, kp)], kbuf.at[pl.ds(i * kp, kp)], sem_k.at[i])

    def v_copy(l, i):
        return pltpu.make_async_copy(vc_hbm.at[l, pl.ds(tok0 + i * kp, kp)], vbuf.at[pl.ds(i * kp, kp)], sem_v.at[i])

    def w_copy(l, i):
        src = (wq_hbm, wk_hbm, wv_hbm, wo_hbm)[i]
        dst = (wqb, wkb, wvb, wob)[i]
        return pltpu.make_async_copy(src.at[l], dst, sem_w.at[i])

    n13 = ff // NW
    npass = nloc * HALVES
    tot13 = layers * npass * n13
    tot2 = layers * nloc

    def g_copies(t):
        lq = lax.div(t, n13)
        j = lax.rem(t, n13)
        l = lax.div(lq, npass)
        i = lax.div(lax.rem(lq, npass), HALVES)
        slot = lax.rem(t, R13)
        cols = pl.ds(pl.multiple_of(j * NW, NW), NW)
        return (pltpu.make_async_copy(wg_hbm.at[l, i, :, cols], w13.at[slot, :, pl.ds(0, NW)], sem_g.at[slot]),
                pltpu.make_async_copy(wu_hbm.at[l, i, :, cols], w13.at[slot, :, pl.ds(NW, NW)], sem_u.at[slot]))

    def d_copy(t):
        return pltpu.make_async_copy(wd_hbm.at[t // nloc, t % nloc], w2b, sem_d.at[0])

    x_copy = pltpu.make_async_copy(x_hbm.at[pl.ds(tok0, tok)], xin, sem_x.at[0])
    x_copy.start()
    for i in range(3):
        w_copy(0, i).start()
    for i in range(kpieces):
        k_copy(0, i).start()

    lane = lax.broadcasted_iota(jnp.int32, (tok, hd), 1)
    pos_i = jnp.zeros((tok, hd), jnp.int32)
    row_i = lax.broadcasted_iota(jnp.int32, (tok, hd), 0)
    for t in range(tok):
        pos_i = jnp.where(row_i == t, len_ref[pool * tok + t], pos_i)
    half_hd = hd // 2
    pair = jnp.where(lane < half_hd, lane, lane - half_hd).astype(F32)
    freqs = jnp.exp(pair * (-2.0 / hd) * jnp.log(jnp.full((tok, hd), ROPE_BASE, F32)))
    angle = pos_i.astype(F32) * freqs
    cos_scr[...] = jnp.cos(angle)
    sn = jnp.sin(angle)
    sin_scr[...] = jnp.where(lane < half_hd, -sn, sn)
    for l in range(layers):
        w = wr_ref[l]
        hi = w.astype(BF16)
        r1 = w - hi.astype(F32)
        mid = r1.astype(BF16)
        lo = (r1 - mid.astype(F32)).astype(BF16)
        wr3[l, pl.ds(0, nexp), :] = hi
        wr3[l, pl.ds(nexp, nexp), :] = mid
        wr3[l, pl.ds(2 * nexp, nexp), :] = lo
    zero_rows = jnp.zeros((ht, hd), F32)
    for h in range(heads, HP):
        q_scr[pl.ds(h, ht, stride=HP), :] = zero_rows
        kn_scr[pl.ds(h, ht, stride=HP), :] = zero_rows
        vn_scr[pl.ds(h, ht, stride=HP), :] = zero_rows

    pl.semaphore_wait(barrier, 7)
    x_copy.wait()
    xs[...] = xin[...].astype(F32)

    scale = hd ** -0.5
    rix = lax.broadcasted_iota(jnp.int32, (HP, seq * kvh), 0)
    cix = lax.broadcasted_iota(jnp.int32, (HP, seq * kvh), 1)
    own_kv = lax.rem(cix, kvh) == lax.div(rix, group)
    colpos = jnp.where(own_kv, lax.div(cix, kvh), 2 * seq)

    def blk(hf, i):
        return pl.ds(pl.multiple_of(hf * hrows + i * ht, ht), ht)

    def hblk(hf, i, s):
        return pl.ds(pl.multiple_of(hf * hrows + i * ht + s * half, half), half)

    hp_pieces = kpieces // HALVES

    def attention(l, hf, hooks):
        trow = slice(hf * ht, (hf + 1) * ht)

        def rotate(v):
            return v * cos_scr[trow, :] + pltpu.roll(v, half_hd, 1) * sin_scr[trow, :]

        def first(i):
            if hf == 0:
                w_copy(l, i).wait()

        xf32 = xs[trow, :]
        h = (xf32 * lax.rsqrt(jnp.mean(xf32 * xf32, axis=-1, keepdims=True) + EPSILON)).astype(BF16)
        first(0)
        per = 256 // hd
        for n in range(heads // per):
            qn = jnp.dot(h, wqb[:, n * 256:(n + 1) * 256], preferred_element_type=F32)
            for s in range(per):
                r = rotate(qn[:, s * hd:(s + 1) * hd]).astype(BF16).astype(F32)
                q_scr[pl.ds(n * per + s, ht, stride=HP), :] = r
        first(1)
        kn = jnp.dot(h, wkb[...], preferred_element_type=F32)
        first(2)
        vn = jnp.dot(h, wvb[...], preferred_element_type=F32)
        for kv in range(kvh):
            r = rotate(kn[:, kv * hd:(kv + 1) * hd]).astype(BF16).astype(F32)
            v = vn[:, kv * hd:(kv + 1) * hd].astype(BF16).astype(F32)
            for g in range(group):
                kn_scr[pl.ds(kv * group + g, ht, stride=HP), :] = r
                vn_scr[pl.ds(kv * group + g, ht, stride=HP), :] = v
        if l == 0 and hf == 0:
            for i in range(kpieces):
                v_copy(l, i).start()
            w_copy(l, 3).start()

        def qk(i, carry):
            for t in range(ht):
                r16 = pl.ds(pl.multiple_of(t * HP, HP), HP)
                q = q_scr[r16, :].astype(BF16)
                sc = lax.dot_general(q, kbuf[hf * ht + t], (((1,), (1,)), ((), ())), preferred_element_type=F32)
                s_scr[r16, :] = jnp.where(colpos < len_ref[pool * tok + hf * ht + t], sc * scale, -jnp.inf)
            return carry

        for i in range(hp_pieces):
            k_copy(l, hf * hp_pieces + i).wait()
        qk(0, 0)
        hooks[0]()
        if l == 0 and hf == 0:
            for t in range(R13):
                for cp in g_copies(t):
                    cp.start()

        def soft(i, carry):
            rr = pl.ds(pl.multiple_of(i * 128, 128), 128)
            sc = s_scr[rr, :]
            s_new = jnp.sum(q_scr[rr, :] * kn_scr[rr, :], axis=-1, keepdims=True) * scale
            peak = jnp.maximum(jnp.max(sc, axis=-1, keepdims=True), s_new)
            wts = jnp.exp(sc - peak)
            w_new = jnp.exp(s_new - peak)
            den = jnp.sum(wts, axis=-1, keepdims=True) + w_new
            p_scr[rr, :] = wts.astype(BF16)
            mn_scr[rr, :] = w_new.astype(BF16).astype(F32) * vn_scr[rr, :]
            den_scr[rr, :] = jnp.broadcast_to(den, (128, hd))
            return carry

        lax.fori_loop(0, ht * HP // 128, soft, 0)
        hooks[1]()

        def pv(i, carry):
            for t in range(ht):
                r16 = pl.ds(pl.multiple_of(t * HP, HP), HP)
                m = jnp.dot(p_scr[r16, :], vbuf[hf * ht + t], preferred_element_type=F32)
                mn_scr[r16, :] = ((m + mn_scr[r16, :]) / den_scr[r16, :]).astype(BF16).astype(F32)
            return carry

        for i in range(hp_pieces):
            v_copy(l, hf * hp_pieces + i).wait()
        pv(0, 0)
        att = jnp.concatenate([mn_scr[pl.ds(h, ht, stride=HP), :].astype(BF16) for h in range(heads)], axis=1)
        first(3)
        for n in range(model // 256):
            cs = slice(n * 256, (n + 1) * 256)
            a_scr[trow, cs] = (xs[trow, cs] + jnp.dot(att, wob[:, cs], preferred_element_type=F32)).astype(BF16).astype(F32)
        a = a_scr[trow, :]
        u = (a * lax.rsqrt(jnp.mean(a * a, axis=-1, keepdims=True) + EPSILON)).astype(BF16)
        u_all[blk(hf, e), :] = u
        parts = lax.dot_general(wr3[l], u, (((1,), (1,)), ((), ())), preferred_element_type=F32)
        logits = (parts[2 * nexp:3 * nexp] + parts[nexp:2 * nexp]) + parts[0:nexp]
        ids = ids_ref[l]
        mine = ids[:, hf * ht:(hf + 1) * ht]
        for i in range(1, npool):
            mine = jnp.where(pool == i, ids[:, i * tok + hf * ht:i * tok + (hf + 1) * ht], mine)
        eix = lax.broadcasted_iota(jnp.int32, (nexp, ht), 0)
        hit = eix == mine[0:1, :]
        for k in range(1, topk):
            hit = jnp.logical_or(hit, eix == mine[k:k + 1, :])
        ml = jnp.where(hit, logits, -jnp.inf)
        ex = jnp.exp(ml - jnp.max(ml, axis=0, keepdims=True))
        gates = ex / jnp.sum(ex, axis=0, keepdims=True)
        g_all[hf, e] = jnp.concatenate([gates, jnp.zeros((nexp, LANES - ht), F32)], axis=1)

    def dcopies(hf, i):
        dev = to_ep((partner, er, el, er, el, partner, partner, dr, dl)[i])
        rws = (blk(hf, e), blk(hf, e), blk(hf, e), hblk(hf, el, 0), hblk(hf, er, 1), blk(hf, el), blk(hf, er),
               hblk(hf, el, 0), hblk(hf, er, 1))[i]
        gix = (e, e, e, el, None, el, er, el, None)[i]
        a = pltpu.make_async_remote_copy(src_ref=u_all.at[rws], dst_ref=u_all.at[rws], send_sem=du_s.at[hf, i],
                                         recv_sem=du_r.at[hf, i], device_id=dev, device_id_type=MESH)
        if gix is None:
            return (a,)
        b = pltpu.make_async_remote_copy(src_ref=g_all.at[hf, gix], dst_ref=g_all.at[hf, gix], send_sem=dg_s.at[hf, i],
                                         recv_sem=dg_r.at[hf, i], device_id=dev, device_id_type=MESH)
        return (a, b)

    def start(cs):
        for cp in cs:
            cp.start()

    def wait_recv(cs):
        for cp in cs:
            cp.wait_recv()

    def wait_send(cs):
        for cp in cs:
            cp.wait_send()

    def disp1(hf):
        for i in (1, 2, 0):
            start(dcopies(hf, i))

    def disp2(hf):
        for i, js in ((1, (3, 7, 5)), (2, (4, 8, 6))):
            wait_recv(dcopies(hf, i))
            for j in js:
                start(dcopies(hf, j))

    def disp3(hf):
        for i in (0, 3, 4, 5, 6, 7, 8):
            wait_recv(dcopies(hf, i))
        for i in range(9):
            wait_send(dcopies(hf, i))
        gt = jnp.transpose(g_all[hf].reshape(ep * nexp, LANES))
        gt = gt[0:ht, :]
        lix = lax.broadcasted_iota(jnp.int32, (ht, ep * nexp), 1)
        for i in range(nloc):
            for b in range(ep):
                col = jnp.sum(jnp.where(lix == b * nexp + e * nloc + i, gt, 0.0), axis=1, keepdims=True)
                gcol[i, pl.ds(hf * hrows + b * ht, ht), :] = jnp.broadcast_to(col, (ht, LANES))

    def experts(l, i, hf, hooks):
        base13 = (l * npass + i * HALVES + hf) * n13
        t2 = l * nloc + i
        rws = slice(hf * hrows, (hf + 1) * hrows)

        def up(j, carry):
            t = base13 + j
            slot = lax.rem(t, R13)
            for cp in g_copies(t):
                cp.wait()
            hh = jnp.dot(u_all[rws, :], w13[slot], preferred_element_type=F32)
            gate = hh[:, 0:NW]
            act = gate * jax.nn.sigmoid(gate) * hh[:, NW:2 * NW]
            inner[:, pl.ds(pl.multiple_of(j * NW, NW), NW)] = act.astype(BF16)

            @pl.when(t + R13 < tot13)
            def _():
                for cp in g_copies(t + R13):
                    cp.start()
            for at, fn in hooks:
                pl.when(j == at)(fn)
            return carry

        lax.fori_loop(0, n13, up, 0)

        if hf == 0:
            d_copy(t2).wait()
        y = jnp.dot(inner[...], w2b[...], preferred_element_type=F32).astype(BF16).astype(F32)
        gc = gcol[i, rws, :]
        for s in range(model // LANES):
            cols = slice(s * LANES, (s + 1) * LANES)
            term = jnp.where(gc > 0.0, gc * y[:, cols], 0.0)
            if i == 0:
                psum[rws, cols] = term
            else:
                psum[rws, cols] = psum[rws, cols] + term
        if hf == HALVES - 1 and t2 + 1 < tot2:
            d_copy(t2 + 1).start()

    order = (xf, xr, xl, xx)

    def pcopy(hf, k):
        return pltpu.make_async_remote_copy(src_ref=psum.at[blk(hf, order[k] * CORES + oc)], dst_ref=pairbuf.at[hf, k],
                                            send_sem=pr_s.at[hf, k], recv_sem=pr_r.at[hf, k], device_id=to_ep(partner),
                                            device_id_type=MESH)

    def rcopy(hf, i):
        rws = (hblk(hf, ef, 1), hblk(hf, ef, 0), hblk(hf, er, 0), hblk(hf, el, 1), hblk(hf, er, 1), hblk(hf, el, 0))[i]
        return pltpu.make_async_remote_copy(src_ref=psum.at[rws], dst_ref=rbuf.at[hf, i], send_sem=rr_s.at[hf, i],
                                            recv_sem=rr_r.at[hf, i], device_id=to_ep(er if i % 2 == 0 else el), device_id_type=MESH)

    def ret1(hf):
        for k in range(nx):
            pcopy(hf, k).start()

    def ret2(hf, ks):
        for k in ks:
            pcopy(hf, k).wait_recv()
            rws = blk(hf, order[k] * CORES + c)
            psum[rws, :] = psum[rws, :] + pairbuf[hf, k]
            for m in ((0, 1), (2,), (3,), ())[k]:
                rcopy(hf, m).start()

    def ret3(hf):
        for m, rws, nxt in ((0, hblk(hf, er, 1), 4), (1, hblk(hf, el, 0), 5)):
            rcopy(hf, m).wait_recv()
            psum[rws, :] = psum[rws, :] + rbuf[hf, m]
            rcopy(hf, nxt).start()

    def ret4(hf):
        for s, m, n in ((0, 2, 5), (1, 3, 4)):
            rcopy(hf, m).wait_recv()
            rcopy(hf, n).wait_recv()
            part = psum[hblk(hf, e, s), :] + rbuf[hf, m] + rbuf[hf, n]
            tr = slice(hf * ht + s * half, hf * ht + (s + 1) * half)
            xs[tr, :] = (a_scr[tr, :] + part).astype(BF16).astype(F32)
        for k in range(nx):
            pcopy(hf, k).wait_send()
        for m in range(6):
            rcopy(hf, m).wait_send()

    def fblk(hf, i):
        return pl.ds(pl.multiple_of(i * tok + hf * ht, ht), ht)

    def fhblk(hf, i, s):
        return pl.ds(pl.multiple_of(i * tok + hf * ht + s * half, half), half)

    def fcopy(hf, i):
        rws = (fblk(hf, pool), fblk(hf, pool), fhblk(hf, pp, 0), fhblk(hf, pn, 1))[i]
        return pltpu.make_async_remote_copy(src_ref=fin.at[rws], dst_ref=fin.at[rws], send_sem=fs.at[hf, i], recv_sem=fr.at[hf, i],
                                            device_id=to_pool(pn if i % 2 == 0 else pp), device_id_type=MESH)

    def ocopy(hf, k):
        i = (pool, pp, pn, pf)[k]
        return pltpu.make_async_copy(fin.at[fblk(hf, i)], out_hbm.at[fblk(hf, i)], sem_o.at[hf, k])

    def fin1(hf):
        fin[fblk(hf, pool), :] = xs[hf * ht:(hf + 1) * ht, :].astype(BF16)
        fcopy(hf, 0).start()
        fcopy(hf, 1).start()
        ocopy(hf, 0).start()

    def fin2(hf):
        for i in range(2):
            fcopy(hf, i).wait_recv()
            fcopy(hf, i + 2).start()
            ocopy(hf, i + 1).start()

    def fin3(hf):
        fcopy(hf, 2).wait_recv()
        fcopy(hf, 3).wait_recv()
        ocopy(hf, 3).start()
        for k in range(4):
            ocopy(hf, k).wait()
            fcopy(hf, k).wait_send()

    def nothing():
        pass

    for l in range(layers):
        attention(l, 0, (nothing if l == 0 else lambda: ret3(1), nothing))
        disp1(0)
        if l > 0:
            ret4(1)
        attention(l, 1, (lambda: disp2(0), nothing))
        disp1(1)
        if l == 0:
            d_copy(0).start()
        disp3(0)
        experts(l, 0, 0, ((n13 - 3, lambda: disp2(1)),))
        if l + 1 < layers:
            for k in range(4):
                w_copy(l + 1, k).start()
            for k in range(kpieces):
                k_copy(l + 1, k).start()
                v_copy(l + 1, k).start()
        disp3(1)
        experts(l, 0, 1, ())
        experts(l, 1, 0, ())
        ret1(0)
        experts(l, 1, 1, ((1, lambda: ret2(0, (0,))), (2, lambda: ret2(0, (1, 2, 3))), (n13 - 1, lambda: ret3(0))))
        ret1(1)
        ret2(1, (0,))
        ret4(0)
        if l + 1 == layers:
            fin1(0)
        ret2(1, (1, 2, 3))
    ret3(1)
    fin2(0)
    ret4(1)
    fin1(1)
    fin3(0)
    fin2(1)
    fin3(1)


def solution(mesh):
    npool = mesh.shape["pool"]
    ep = mesh.shape["ep"]
    nx = ep // CORES

    def body(hidden, k_cache, v_cache, lengths, expert_ids, w_query, w_key, w_value, w_out, w_router, w_gate, w_up, w_down):
        layers, local, seq, kvh, hd = k_cache.shape
        model = hidden.shape[1]
        tok = local // npool
        heads = w_query.shape[2] // hd
        nloc, _, ff = w_gate.shape[1:]
        nexp = w_router.shape[2]
        topk = expert_ids.shape[2]
        kc = k_cache.reshape(layers, local, seq * kvh, hd)
        vc = v_cache.reshape(layers, local, seq * kvh, hd)
        ids_t = expert_ids.transpose(0, 2, 1)
        wr_t = w_router.transpose(0, 2, 1)
        cfg = (layers, tok, model, heads, kvh, hd, seq, ff, nloc, nx, npool, nexp, topk)
        rows = ep * tok
        ht = tok // HALVES
        hbm = pl.BlockSpec(memory_space=pl.ANY)
        vmem = pl.BlockSpec(memory_space=pltpu.VMEM)
        smem = pl.BlockSpec(memory_space=pltpu.SMEM)
        kpieces = 8
        dma = pltpu.SemaphoreType.DMA
        scratch = [
            pltpu.VMEM((tok, model), BF16), pltpu.VMEM((tok, model), F32), pltpu.VMEM((tok, model), F32),
            pltpu.VMEM((ht * HP, hd), F32), pltpu.VMEM((ht * HP, hd), F32), pltpu.VMEM((ht * HP, hd), F32),
            pltpu.VMEM((ht * HP, hd), F32), pltpu.VMEM((ht * HP, hd), F32),
            pltpu.VMEM((ht * HP, seq * kvh), F32), pltpu.VMEM((ht * HP, seq * kvh), BF16),
            pltpu.VMEM((tok, hd), F32), pltpu.VMEM((tok, hd), F32), pltpu.VMEM((layers, 3 * nexp, model), BF16),
            pltpu.VMEM((tok, seq * kvh, hd), BF16), pltpu.VMEM((tok, seq * kvh, hd), BF16),
            pltpu.VMEM((model, heads * hd), BF16), pltpu.VMEM((model, kvh * hd), BF16), pltpu.VMEM((model, kvh * hd), BF16),
            pltpu.VMEM((heads * hd, model), BF16),
            pltpu.VMEM((R13, model, 2 * NW), BF16), pltpu.VMEM((ff, model), BF16),
            pltpu.VMEM((rows, model), BF16), pltpu.VMEM((HALVES, ep, nexp, LANES), F32), pltpu.VMEM((nloc, rows, LANES), F32),
            pltpu.VMEM((rows // HALVES, ff), BF16), pltpu.VMEM((rows, model), F32), pltpu.VMEM((HALVES, nx, ht, model), F32),
            pltpu.VMEM((HALVES, 6, ht // 2, model), F32), pltpu.VMEM((local, model), BF16),
            dma((1,)), dma((4,)), dma((kpieces,)), dma((kpieces,)), dma((R13,)), dma((R13,)), dma((1,)),
            dma((HALVES, 9)), dma((HALVES, 9)), dma((HALVES, 9)), dma((HALVES, 9)), dma((HALVES, nx)), dma((HALVES, nx)),
            dma((HALVES, 6)), dma((HALVES, 6)), dma((HALVES, 4)), dma((HALVES, 4)), dma((HALVES, npool)),
        ]
        call = pl.pallas_call(
            functools.partial(step_kernel, cfg),
            out_shape=jax.ShapeDtypeStruct((local, model), BF16),
            in_specs=[hbm, hbm, hbm, smem, vmem, hbm, hbm, hbm, hbm, vmem, hbm, hbm, hbm],
            out_specs=hbm,
            scratch_shapes=scratch,
            compiler_params=pltpu.CompilerParams(collective_id=0, has_side_effects=True, vmem_limit_bytes=66_000_000),
        )
        return call(hidden, kc, vc, lengths, ids_t, w_query, w_key, w_value, w_out, wr_t, w_gate, w_up, w_down)

    rows_spec = ("dp", "ep")
    in_specs = (P(rows_spec, None), P(None, rows_spec), P(None, rows_spec), P(rows_spec), P(None, rows_spec, None), P(), P(), P(), P(), P(), P(None, "ep"), P(None, "ep"), P(None, "ep"))
    return jax.shard_map(body, mesh=mesh, in_specs=in_specs, out_specs=P(rows_spec, None), check_vma=False)
```

time: 158 us -> 134 us (0.85)
  Pallas kernels: 154 us -> 132 us
    pallas_call x1, Pallas kernels: 154 us -> 132 us  [body(): call(hidden, kc, vc, lengths, ids_t, w_query, w_key, w_value, w_out, wr_t...]
where the time goes in v2:
time: 134 us
  Pallas kernels  132 us (99%)
  local copies, waits for them, and re-layouts  2.06 us (2%)
    pallas_call x1, Pallas kernels, body(): call(hidden, kc, vc, lengths, ids_t, w_query, w_key, w_value, w_out, wr_t...  132 us

profile of v2, /device:TPU:97, one launch (start us, length us, event | category | flops | bytes accessed | tf_op | source)
XLA Modules:
  0.0 134.0 jit_solution(17170281484728953133)
XLA Ops:
  0.0 132.0 %shard_map.127 = bf16[256,1536]{1,0:T(8,128)(2,1)} custom-call(bf16[256,1536]{1,0:T(8,128)(2,1)} %x_hbm.1, bf16[2,256,256,128]{3,2,1,0:T(8,128)(2,1)} %bitcast.4, bf16[2,256,256,128]{3,2,1,0:T(8,128)(2,1)} %bitcast.5, s32[256]{0:T(256)} %len_ref.1, s32[2,4,256]{2,1,0:T(4,128)} %bitcast.7, bf16[2,1536,1536]{2,1,0:T(8,128)(2,1)} %wq_hbm.1, ...), custom_call_target="tpu_custom_call" | custom-call | tf_op jit(solution)/shard_map/pallas_call | solution.py:504
  132.0 2.1 %copy.15 = bf16[256,1536]{1,0:T(8,128)(2,1)} copy(bf16[256,1536]{1,0:T(8,128)(2,1)} %shard_map.127) | data formatting | bytes 1572864

commit v3 on v2

--- a/solution.py
+++ b/solution.py
@@ -15,8 +15,7 @@
 CORES = 2
 HP = 16
 LANES = 128
-NW = 384
-R13 = 4
+NW = 896
 HALVES = 2
 
 
@@ -79,21 +78,20 @@
 
     n13 = ff // NW
     npass = nloc * HALVES
-    tot13 = layers * npass * n13
+    tot13 = layers * nloc * n13
     tot2 = layers * nloc
 
     def g_copies(t):
-        lq = lax.div(t, n13)
-        j = lax.rem(t, n13)
-        l = lax.div(lq, npass)
-        i = lax.div(lax.rem(lq, npass), HALVES)
-        slot = lax.rem(t, R13)
-        cols = pl.ds(pl.multiple_of(j * NW, NW), NW)
+        li = lax.div(t, n13)
+        slot = lax.rem(t, n13)
+        l = lax.div(li, nloc)
+        i = lax.rem(li, nloc)
+        cols = pl.ds(pl.multiple_of(slot * NW, NW), NW)
         return (pltpu.make_async_copy(wg_hbm.at[l, i, :, cols], w13.at[slot, :, pl.ds(0, NW)], sem_g.at[slot]),
                 pltpu.make_async_copy(wu_hbm.at[l, i, :, cols], w13.at[slot, :, pl.ds(NW, NW)], sem_u.at[slot]))
 
     def d_copy(t):
-        return pltpu.make_async_copy(wd_hbm.at[t // nloc, t % nloc], w2b, sem_d.at[0])
+        return pltpu.make_async_copy(wd_hbm.at[lax.div(t, nloc), lax.rem(t, nloc)], w2b, sem_d.at[0])
 
     x_copy = pltpu.make_async_copy(x_hbm.at[pl.ds(tok0, tok)], xin, sem_x.at[0])
     x_copy.start()
@@ -176,10 +174,12 @@
             for g in range(group):
                 kn_scr[pl.ds(kv * group + g, ht, stride=HP), :] = r
                 vn_scr[pl.ds(kv * group + g, ht, stride=HP), :] = v
-        if l == 0 and hf == 0:
-            for i in range(kpieces):
-                v_copy(l, i).start()
-            w_copy(l, 3).start()
+        if hf == 0:
+            @pl.when(l == 0)
+            def _():
+                for i in range(kpieces):
+                    v_copy(l, i).start()
+                w_copy(l, 3).start()
 
         def qk(i, carry):
             for t in range(ht):
@@ -193,10 +193,12 @@
             k_copy(l, hf * hp_pieces + i).wait()
         qk(0, 0)
         hooks[0]()
-        if l == 0 and hf == 0:
-            for t in range(R13):
-                for cp in g_copies(t):
-                    cp.start()
+        if hf == 0:
+            @pl.when(l == 0)
+            def _():
+                for t in range(n13):
+                    for cp in g_copies(t):
+                        cp.start()
 
         def soft(i, carry):
             rr = pl.ds(pl.multiple_of(i * 128, 128), 128)
@@ -248,10 +250,10 @@
         g_all[hf, e] = jnp.concatenate([gates, jnp.zeros((nexp, LANES - ht), F32)], axis=1)
 
     def dcopies(hf, i):
-        dev = to_ep((partner, er, el, er, el, partner, partner, dr, dl)[i])
-        rws = (blk(hf, e), blk(hf, e), blk(hf, e), hblk(hf, el, 0), hblk(hf, er, 1), blk(hf, el), blk(hf, er),
-               hblk(hf, el, 0), hblk(hf, er, 1))[i]
-        gix = (e, e, e, el, None, el, er, el, None)[i]
+        dev = to_ep((partner, er, el, er, el, partner, partner, dr, dl, er, el)[i])
+        rws = (blk(hf, e), hblk(hf, e, 0), hblk(hf, e, 1), hblk(hf, el, 0), hblk(hf, er, 1), blk(hf, el), blk(hf, er),
+               hblk(hf, el, 0), hblk(hf, er, 1), hblk(hf, e, 1), hblk(hf, e, 0))[i]
+        gix = (e, e, e, el, None, el, er, el, None, None, None)[i]
         a = pltpu.make_async_remote_copy(src_ref=u_all.at[rws], dst_ref=u_all.at[rws], send_sem=du_s.at[hf, i],
                                          recv_sem=du_r.at[hf, i], device_id=dev, device_id_type=MESH)
         if gix is None:
@@ -273,19 +275,24 @@
             cp.wait_send()
 
     def disp1(hf):
-        for i in (1, 2, 0):
+        for i in (1, 2, 9, 10, 0):
             start(dcopies(hf, i))
 
     def disp2(hf):
-        for i, js in ((1, (3, 7, 5)), (2, (4, 8, 6))):
+        for i, js in ((1, (3, 7)), (2, (4, 8))):
             wait_recv(dcopies(hf, i))
             for j in js:
                 start(dcopies(hf, j))
 
     def disp3(hf):
+        for i, j in ((9, 5), (10, 6)):
+            wait_recv(dcopies(hf, i))
+            start(dcopies(hf, j))
+
+    def disp4(hf):
         for i in (0, 3, 4, 5, 6, 7, 8):
             wait_recv(dcopies(hf, i))
-        for i in range(9):
+        for i in range(11):
             wait_send(dcopies(hf, i))
         gt = jnp.transpose(g_all[hf].reshape(ep * nexp, LANES))
         gt = gt[0:ht, :]
@@ -295,43 +302,49 @@
                 col = jnp.sum(jnp.where(lix == b * nexp + e * nloc + i, gt, 0.0), axis=1, keepdims=True)
                 gcol[i, pl.ds(hf * hrows + b * ht, ht), :] = jnp.broadcast_to(col, (ht, LANES))
 
-    def experts(l, i, hf, hooks):
-        base13 = (l * npass + i * HALVES + hf) * n13
+    def experts(l, q, hooks):
+        i = lax.div(q, HALVES)
+        hf = lax.rem(q, HALVES)
         t2 = l * nloc + i
-        rws = slice(hf * hrows, (hf + 1) * hrows)
+        base13 = t2 * n13
+        rws = pl.ds(pl.multiple_of(hf * hrows, hrows), hrows)
 
         def up(j, carry):
             t = base13 + j
-            slot = lax.rem(t, R13)
-            for cp in g_copies(t):
-                cp.wait()
-            hh = jnp.dot(u_all[rws, :], w13[slot], preferred_element_type=F32)
+
+            @pl.when(hf == 0)
+            def _():
+                for cp in g_copies(t):
+                    cp.wait()
+
+            hh = jnp.dot(u_all[rws, :], w13[j], preferred_element_type=F32)
             gate = hh[:, 0:NW]
             act = gate * jax.nn.sigmoid(gate) * hh[:, NW:2 * NW]
             inner[:, pl.ds(pl.multiple_of(j * NW, NW), NW)] = act.astype(BF16)
 
-            @pl.when(t + R13 < tot13)
+            @pl.when(jnp.logical_and(hf == HALVES - 1, t + n13 < tot13))
             def _():
-                for cp in g_copies(t + R13):
+                for cp in g_copies(t + n13):
                     cp.start()
-            for at, fn in hooks:
-                pl.when(j == at)(fn)
+            for qa, at, fn in hooks:
+                pl.when(jnp.logical_and(q == qa, j == at))(fn)
             return carry
 
         lax.fori_loop(0, n13, up, 0)
 
-        if hf == 0:
+        @pl.when(hf == 0)
+        def _():
             d_copy(t2).wait()
+
         y = jnp.dot(inner[...], w2b[...], preferred_element_type=F32).astype(BF16).astype(F32)
         gc = gcol[i, rws, :]
         for s in range(model // LANES):
             cols = slice(s * LANES, (s + 1) * LANES)
             term = jnp.where(gc > 0.0, gc * y[:, cols], 0.0)
-            if i == 0:
-                psum[rws, cols] = term
-            else:
-                psum[rws, cols] = psum[rws, cols] + term
-        if hf == HALVES - 1 and t2 + 1 < tot2:
+            psum[rws, cols] = jnp.where(i == 0, 0.0, psum[rws, cols]) + term
+
+        @pl.when(jnp.logical_and(hf == HALVES - 1, t2 + 1 < tot2))
+        def _():
             d_copy(t2 + 1).start()
 
     order = (xf, xr, xl, xx)
@@ -383,7 +396,7 @@
         return pl.ds(pl.multiple_of(i * tok + hf * ht + s * half, half), half)
 
     def fcopy(hf, i):
-        rws = (fblk(hf, pool), fblk(hf, pool), fhblk(hf, pp, 0), fhblk(hf, pn, 1))[i]
+        rws = (fhblk(hf, pool, 0), fhblk(hf, pool, 1), fhblk(hf, pp, 0), fhblk(hf, pn, 1), fhblk(hf, pool, 1), fhblk(hf, pool, 0))[i]
         return pltpu.make_async_remote_copy(src_ref=fin.at[rws], dst_ref=fin.at[rws], send_sem=fs.at[hf, i], recv_sem=fr.at[hf, i],
                                             device_id=to_pool(pn if i % 2 == 0 else pp), device_id_type=MESH)
 
@@ -393,14 +406,16 @@
 
     def fin1(hf):
         fin[fblk(hf, pool), :] = xs[hf * ht:(hf + 1) * ht, :].astype(BF16)
-        fcopy(hf, 0).start()
-        fcopy(hf, 1).start()
+        for i in (0, 1, 4, 5):
+            fcopy(hf, i).start()
         ocopy(hf, 0).start()
 
     def fin2(hf):
         for i in range(2):
             fcopy(hf, i).wait_recv()
             fcopy(hf, i + 2).start()
+        for i in range(2):
+            fcopy(hf, i + 4).wait_recv()
             ocopy(hf, i + 1).start()
 
     def fin3(hf):
@@ -409,39 +424,51 @@
         ocopy(hf, 3).start()
         for k in range(4):
             ocopy(hf, k).wait()
+        for k in range(6):
             fcopy(hf, k).wait_send()
 
     def nothing():
         pass
 
-    for l in range(layers):
-        attention(l, 0, (nothing if l == 0 else lambda: ret3(1), nothing))
+    def layer(l, carry):
+        later = l > 0
+        last = l == layers - 1
+
+        attention(l, 0, (lambda: pl.when(later)(lambda: ret3(1)), nothing))
         disp1(0)
-        if l > 0:
-            ret4(1)
-        attention(l, 1, (lambda: disp2(0), nothing))
+        pl.when(later)(lambda: ret4(1))
+        attention(l, 1, (lambda: disp2(0), lambda: disp3(0)))
         disp1(1)
-        if l == 0:
-            d_copy(0).start()
-        disp3(0)
-        experts(l, 0, 0, ((n13 - 3, lambda: disp2(1)),))
-        if l + 1 < layers:
+        pl.when(l == 0)(lambda: d_copy(0).start())
+        disp4(0)
+
+        def next_loads():
             for k in range(4):
                 w_copy(l + 1, k).start()
             for k in range(kpieces):
                 k_copy(l + 1, k).start()
                 v_copy(l + 1, k).start()
-        disp3(1)
-        experts(l, 0, 1, ())
-        experts(l, 1, 0, ())
-        ret1(0)
-        experts(l, 1, 1, ((1, lambda: ret2(0, (0,))), (2, lambda: ret2(0, (1, 2, 3))), (n13 - 1, lambda: ret3(0))))
+
+        end = npass - 1
+        hooks = ((0, n13 - 2, lambda: disp2(1)), (0, n13 - 1, lambda: disp3(1)), (end, 0, lambda: ret2(0, (0,))),
+                 (end, n13 - 2, lambda: ret2(0, (1, 2, 3))), (end, n13 - 1, lambda: ret3(0)))
+
+        def one_pass(q, c2):
+            pl.when(q == 1)(lambda: disp4(1))
+            pl.when(q == end)(lambda: ret1(0))
+            experts(l, q, hooks)
+            pl.when(jnp.logical_and(q == 0, l + 1 < layers))(next_loads)
+            return c2
+
+        lax.fori_loop(0, npass, one_pass, 0)
         ret1(1)
         ret2(1, (0,))
         ret4(0)
-        if l + 1 == layers:
-            fin1(0)
+        pl.when(last)(lambda: fin1(0))
         ret2(1, (1, 2, 3))
+        return carry
+
+    lax.fori_loop(0, layers, layer, 0)
     ret3(1)
     fin2(0)
     ret4(1)
@@ -485,13 +512,13 @@
             pltpu.VMEM((tok, seq * kvh, hd), BF16), pltpu.VMEM((tok, seq * kvh, hd), BF16),
             pltpu.VMEM((model, heads * hd), BF16), pltpu.VMEM((model, kvh * hd), BF16), pltpu.VMEM((model, kvh * hd), BF16),
             pltpu.VMEM((heads * hd, model), BF16),
-            pltpu.VMEM((R13, model, 2 * NW), BF16), pltpu.VMEM((ff, model), BF16),
+            pltpu.VMEM((ff // NW, model, 2 * NW), BF16), pltpu.VMEM((ff, model), BF16),
             pltpu.VMEM((rows, model), BF16), pltpu.VMEM((HALVES, ep, nexp, LANES), F32), pltpu.VMEM((nloc, rows, LANES), F32),
             pltpu.VMEM((rows // HALVES, ff), BF16), pltpu.VMEM((rows, model), F32), pltpu.VMEM((HALVES, nx, ht, model), F32),
             pltpu.VMEM((HALVES, 6, ht // 2, model), F32), pltpu.VMEM((local, model), BF16),
-            dma((1,)), dma((4,)), dma((kpieces,)), dma((kpieces,)), dma((R13,)), dma((R13,)), dma((1,)),
-            dma((HALVES, 9)), dma((HALVES, 9)), dma((HALVES, 9)), dma((HALVES, 9)), dma((HALVES, nx)), dma((HALVES, nx)),
-            dma((HALVES, 6)), dma((HALVES, 6)), dma((HALVES, 4)), dma((HALVES, 4)), dma((HALVES, npool)),
+            dma((1,)), dma((4,)), dma((kpieces,)), dma((kpieces,)), dma((ff // NW,)), dma((ff // NW,)), dma((1,)),
+            dma((HALVES, 11)), dma((HALVES, 11)), dma((HALVES, 11)), dma((HALVES, 11)), dma((HALVES, nx)), dma((HALVES, nx)),
+            dma((HALVES, 6)), dma((HALVES, 6)), dma((HALVES, 6)), dma((HALVES, 6)), dma((HALVES, npool)),
         ]
         call = pl.pallas_call(
             functools.partial(step_kernel, cfg),

time: 134 us -> 126 us (0.940)
  Pallas kernels: 132 us -> 124 us
    pallas_call x1, Pallas kernels: 132 us -> 124 us  [body(): call(hidden, kc, vc, lengths, ids_t, w_query, w_key, w_value, w_out, wr_t...]
where the time goes in v3:
time: 126 us
  Pallas kernels  124 us (98%)
  local copies, waits for them, and re-layouts  2.06 us (2%)
    pallas_call x1, Pallas kernels, body(): call(hidden, kc, vc, lengths, ids_t, w_query, w_key, w_value, w_out, wr_t...  124 us

profile of v3, /device:TPU:97, one launch (start us, length us, event | category | flops | bytes accessed | tf_op | source)
XLA Modules:
  0.0 125.7 jit_solution(5498741117373584612)
XLA Ops:
  0.0 123.6 %shard_map.127 = bf16[256,1536]{1,0:T(8,128)(2,1)} custom-call(bf16[256,1536]{1,0:T(8,128)(2,1)} %x_hbm.1, bf16[2,256,256,128]{3,2,1,0:T(8,128)(2,1)} %bitcast.4, bf16[2,256,256,128]{3,2,1,0:T(8,128)(2,1)} %bitcast.5, s32[256]{0:T(256)} %len_ref.1, s32[2,4,256]{2,1,0:T(4,128)} %bitcast.7, bf16[2,1536,1536]{2,1,0:T(8,128)(2,1)} %wq_hbm.1, ...), custom_call_target="tpu_custom_call" | custom-call | tf_op jit(solution)/shard_map/pallas_call | solution.py:531
  123.6 2.1 %copy.15 = bf16[256,1536]{1,0:T(8,128)(2,1)} copy(bf16[256,1536]{1,0:T(8,128)(2,1)} %shard_map.127) | data formatting | bytes 1572864
